TPU v7x, 32 devices: a whole 2x2x4 slice. The times are simulated.
32 devices in a mesh: grp: 2 (over y), seq: 4 (over z), head: 2 (over x), sub: 2 (over core).
Axes of the slice: x: 2, y: 2, z: 4, core: 2. Of those that a mesh axis runs over, the one named last changes fastest.
Arguments:
- latents: bfloat16 [8, 256, 1152], P(('grp', 'seq'), ('head', 'sub')), parts along dimension 0, may hold values from -6 to 6
- timestep: int32 [2], P('grp'), parts along dimension 0, may hold values from 0 to 29
- time_table: float32 [30, 3, 1152], replicated, may hold values from -3 to 3
- shift_table: float32 [2, 3, 1152], replicated, may hold values from -2 to 2
- qkv_weight: bfloat16 [2, 1152, 16, 216], P(None, None, ('head', 'sub')), may hold values from -0.1875 to 0.1875
- norm_gains: float32 [2, 2, 72], replicated, may hold values from 0.1 to 1.9
- out_weight: bfloat16 [2, 1152, 1152], P(None, ('head', 'sub')), may hold values from -0.1875 to 0.1875
Outputs:
- mixed: bfloat16 [8, 256, 1152], P(('grp', 'seq'), ('head', 'sub')), parts along dimension 0
There are 2 independent parts, one for each index of `grp`. A program takes and returns all parts, laid end to end along the dimension named above; an argument that names none is the same for every part. Nothing has to cross between parts.
All inputs are finite; a program needn't handle non-finite values.
Results may differ from a plain program's by a relative error of at most 0.0095.
Values may be sent and summed in bfloat16 or wider, within the bound.
No kernel may reach another device: no remote copies, remote signals or barrier semaphores. Data moves between devices by JAX's collectives and lax.ppermute only.
A program may use at most 64 MiB of HBM per device.

v0:
```python
import jax
import jax.numpy as jnp
from jax import lax
from jax.sharding import PartitionSpec as P

EPSILON = 1e-06


def modulate(values, shift_row, scale_row):
    widened = values.astype(jnp.float32)
    center = jnp.mean(widened, axis=-1, keepdims=True)
    spread = jnp.mean(jnp.square(widened - center), axis=-1, keepdims=True)
    normal = (widened - center) * lax.rsqrt(spread + EPSILON)
    return (normal * (1.0 + scale_row) + shift_row).astype(jnp.bfloat16)


def rms_gain(values, gain_row):
    return (
        values
        * lax.rsqrt(jnp.mean(jnp.square(values), axis=-1, keepdims=True) + EPSILON)
        * gain_row
    )


def project(normed, weight, gain_pair):
    leading = normed.shape[:-1]
    head_count = weight.shape[1]
    head_dim = weight.shape[2] // 3
    flattened = jnp.dot(
        normed.reshape(-1, normed.shape[-1]),
        weight.reshape(weight.shape[0], -1),
        preferred_element_type=jnp.float32,
    )
    pieces = flattened.reshape(leading + (head_count, 3, head_dim))
    queries = rms_gain(pieces[..., 0, :], gain_pair[0])
    key_part = rms_gain(pieces[..., 1, :], gain_pair[1])
    return jnp.concatenate([queries, key_part, pieces[..., 2, :]], axis=-1).astype(jnp.bfloat16)


def attend(packed):
    head_dim = packed.shape[-1] // 3
    queries = packed[..., :head_dim]
    key_part = packed[..., head_dim : 2 * head_dim]
    value_part = packed[..., 2 * head_dim :]
    count = queries.shape[0]
    block = 512 if count % 512 == 0 else count
    blocks = queries.reshape((count // block, block) + queries.shape[1:])

    def one_block(query_block):
        scores = jnp.einsum(
            "qhd,khd->hqk", query_block, key_part, preferred_element_type=jnp.float32
        ) * head_dim ** (-0.5)
        exponent = jnp.exp(scores)
        weights = (exponent / jnp.sum(exponent, axis=-1, keepdims=True)).astype(jnp.bfloat16)
        return jnp.einsum(
            "hqk,khd->qhd", weights, value_part, preferred_element_type=jnp.float32
        ).astype(jnp.bfloat16)

    result = lax.map(one_block, blocks)
    return result.reshape((count,) + result.shape[2:])


def body(latents, timestep, time_table, shift_table, qkv_weight, norm_gains, out_weight):
    feature_width = latents.shape[2]
    chosen = (jnp.arange(time_table.shape[0]) == timestep[0])[:, None, None]
    shared = jnp.sum(jnp.where(chosen, time_table, 0.0), axis=0)
    modulation = shared[None] + shift_table

    def gathered_heads(normed, layer_index):
        return project(
            lax.all_gather(normed, ("head", "sub"), axis=1, tiled=True),
            qkv_weight[layer_index],
            norm_gains[layer_index],
        )

    def back_to_tokens(attended, layer_index):
        merged = attended.reshape(attended.shape[0], attended.shape[1], -1)
        all_heads = lax.all_to_all(merged, ("head", "sub"), split_axis=1, concat_axis=2, tiled=True)
        row_block = all_heads.reshape(-1, all_heads.shape[-1])
        summed = jnp.dot(
            row_block,
            lax.all_gather(out_weight[layer_index], ("head", "sub"), axis=0, tiled=True),
            preferred_element_type=jnp.float32,
        )
        return summed.reshape(all_heads.shape[0], all_heads.shape[1], feature_width)

    normed = modulate(latents, modulation[0, 0], modulation[0, 1])
    packed = gathered_heads(normed, 0)
    attended = lax.map(attend, packed)
    update = back_to_tokens(attended, 0)
    current = (latents.astype(jnp.float32) + modulation[0, 2] * update).astype(jnp.bfloat16)
    shifted_rows = lax.all_to_all(current, "seq", split_axis=1, concat_axis=0, tiled=True)
    packed = gathered_heads(modulate(shifted_rows, modulation[1, 0], modulation[1, 1]), 1)
    attended = jax.vmap(attend, in_axes=1, out_axes=1)(packed)
    update = back_to_tokens(attended, 1)
    result = (shifted_rows.astype(jnp.float32) + modulation[1, 2] * update).astype(jnp.bfloat16)
    return lax.all_to_all(result, "seq", split_axis=0, concat_axis=1, tiled=True)


def solution(mesh):
    return jax.shard_map(
        body,
        mesh=mesh,
        in_specs=(
            P(("grp", "seq"), ("head", "sub"), None),
            P("grp"),
            P(),
            P(),
            P(None, None, ("head", "sub"), None),
            P(),
            P(None, ("head", "sub"), None),
        ),
        out_specs=P(("grp", "seq"), ("head", "sub"), None),
        check_vma=False,
    )
```

profile of v0, /device:TPU:0, one launch (start us, length us, event | category | flops | bytes accessed | tf_op | source)
XLA Modules:
  0.0 99.6 jit_solution(3621725734920662956)
XLA Ops:
  6.5 2.5 %fusion.61 = (bf16[1,288,1152]{2,1,0:T(8,128)(2,1)}, bf16[1,288,1152]{2,1,0:T(8,128)(2,1)}) fusion(bf16[2,288,1152]{2,1,0:T(8,128)(2,1)} %param.13), kind=kLoop, calls=%fused_computation.89 | loop fusion | bytes 2654208 | tf_op jit(solution)/shard_map/slice | solution.py:82
  9.8 0.1 select_reduce_fusion
  10.0 0.1 convert_reduce_fusion
  10.2 0.2 fusion.33
  10.4 0.1 fusion.36
  10.5 9.0 %all_gather.12 = bf16[1,256,1152]{2,1,0:T(8,128)(2,1)S(1)} all-gather(bf16[1,64,1152]{2,1,0:T(8,128)(2,1)S(1)} %fusion.36), channel_id=1, replica_groups=mesh['grp'=2,'seq'=4,'head'=2,'sub'=2] {'head','sub'}, dimensions={1}, use_global_device_ids=true | all-gather | bytes 737280 | tf_op jit(solution)/shard_map/all_gather | solution.py:71
  19.5 4.1 %fusion.60 = (bf16[1,1152,4,216]{1,3,2,0:T(8,128)(2,1)}, bf16[1,1152,4,216]{1,3,2,0:T(8,128)(2,1)S(1)}) fusion(bf16[2,1152,4,216]{1,3,2,0:T(8,128)(2,1)} %param.11), kind=kLoop, calls=%fused_computation.88 | loop fusion | bytes 7962624 | tf_op jit(solution)/shard_map/slice | solution.py:72
  23.6 0.8 convolution_bitcast_fusion
  24.5 0.4 fusion.25
  24.9 0.3 convolution_convert_fusion.1
  25.3 0.4 copy.35
  25.7 0.5 broadcast.178
  26.2 1.9 %reduce.20 = bf16[256,288]{1,0:T(8,128)(2,1)S(1)} reduce(bf16[256,1,288]{2,1,0:T(2,128)(2,1)S(1)} %bitcast.139, bf16[]{:T(256)} %broadcast.178), dimensions={1}, to_apply=%bitcast.118.reduce_sub_computation | reduce | bytes 294914
  28.1 0.3 reshape.234
  28.4 9.1 %all_to_all.51 = bf16[4,2,9216]{2,1,0:T(2,128)(2,1)S(1)} all-to-all(bf16[4,2,9216]{2,1,0:T(2,128)(2,1)S(1)} %reshape.234), channel_id=1, replica_groups=mesh['grp'=2,'seq'=4,'head'=2,'sub'=2] {'head','sub'}, dimensions={0} | all-to-all | bytes 294912 | tf_op jit(solution)/shard_map/all_to_all | solution.py:78
  37.5 0.4 reshape.235
  37.9 0.2 copy.36
  38.0 0.2 reshape.218
  38.2 1.1 %all-gather.5.cloned.1.call-done = bf16[1,1152,1152]{2,1,0:T(8,128)(2,1)} async-done(((bf16[1,288,1152]{2,1,0:T(8,128)(2,1)}), bf16[1,1152,1152]{2,1,0:T(8,128)(2,1)}) %all-gather.5.cloned.1.call-update) | async-done | bytes 2654224 | tf_op jit(solution)/shard_map/all_gather | solution.py:82
  39.3 2.3 %fusion.19 = bf16[1,64,1152]{2,1,0:T(8,128)(2,1)S(1)} fusion(bf16[64,1152]{1,0:T(8,128)(2,1)S(1)} %reshape.218, bf16[1,1152,1152]{2,1,0:T(8,128)(2,1)} %all-gather.5.cloned.1.call-done, bf16[1,64,1152]{2,1,0:T(8,128)(2,1)S(1)} %copy-done, f32[1152]{0:T(1024)S(1)} %get-tuple-element.58), kind=kOutput, calls=%fused_computation.9 | convolution fusion | flops 170164224 | bytes 3101184 | tf_op jit(solution)/shard_map/dot_general | solution.py:80
  41.6 0.2 copy.61
  41.9 1.5 %reduce.21 = bf16[64,1152]{1,0:T(8,128)(2,1)S(1)} reduce(bf16[64,1,1152]{2,1,0:T(2,128)(2,1)S(1)} %bitcast.140, bf16[]{:T(256)} %broadcast.178), dimensions={1}, to_apply=%bitcast.131.reduce_sub_computation | reduce | bytes 294914
  43.4 0.7 reshape.236
  44.1 4.6 %all-to-all-start.1 = ((bf16[4,2,9216]{2,1,0:T(2,128)(2,1)}), bf16[4,2,9216]{2,1,0:T(2,128)(2,1)S(1)}, u32[]{:S(2)}, u32[]{:S(2)}) async-start(bf16[4,2,9216]{2,1,0:T(2,128)(2,1)} %reshape.236), calls=%async_computation.1 | async-start | bytes 294912 | tf_op jit(solution)/shard_map/all_to_all | solution.py:92
  48.7 0.7 all-gather.7.cloned.1.call-update
  49.4 5.8 %all-to-all-done.1 = bf16[4,2,9216]{2,1,0:T(2,128)(2,1)S(1)} async-done(((bf16[4,2,9216]{2,1,0:T(2,128)(2,1)}), bf16[4,2,9216]{2,1,0:T(2,128)(2,1)S(1)}, u32[]{:S(2)}, u32[]{:S(2)}) %all-to-all-start.1) | async-done | bytes 147488 | tf_op jit(solution)/shard_map/all_to_all | solution.py:92
  55.2 0.1 reshape.237
  55.3 0.6 convert_reduce_fusion.1
  55.9 0.1 div.61
  56.0 1.0 %multiply_reduce_fusion.2 = f32[64]{0:T(128)S(1)} fusion(f32[64]{0:T(128)S(1)} %broadcast_multiply_fusion, bf16[64,1,1152]{2,1,0:T(2,128)(2,1)S(1)} %reshape.237), kind=kLoop, calls=%fused_computation.46 | loop fusion | flops 294848 | bytes 147968 | tf_op jit(solution)/shard_map/reduce_sum | solution.py:12
  57.0 0.1 rsqrt.55
  57.1 0.1 add_convert_fusion
  57.2 9.7 %all_gather.14 = bf16[4,64,1152]{2,1,0:T(8,128)(2,1)S(1)} all-gather(bf16[4,16,1152]{2,1,0:T(8,128)(2,1)S(1)} %add_convert_fusion), channel_id=1, replica_groups=mesh['grp'=2,'seq'=4,'head'=2,'sub'=2] {'head','sub'}, dimensions={1}, use_global_device_ids=true | all-gather | bytes 737280 | tf_op jit(solution)/shard_map/all_gather | solution.py:71
  66.9 2.8 %fusion.27 = f32[4,64,4,3,72]{4,1,3,2,0:T(8,128)S(1)} fusion(bf16[4,3,72,1152,1]{3,2,1,0,4:T(8,128)(2,1)} %bitcast.137, bf16[4,64,1152]{2,1,0:T(8,128)(2,1)S(1)} %all_gather.14), kind=kOutput, calls=%fused_computation.18 | convolution fusion | flops 509607936 | bytes 3465216 | tf_op jit(solution)/shard_map/dot_general | solution.py:29
  69.7 0.4 multiply_reduce_fusion.1
  70.1 0.3 fusion.41
  70.5 0.5 fusion.45
  70.9 0.3 copy.40
  71.3 0.3 copy.42
  71.7 0.4 fusion.26
  72.1 0.1 copy.50
  72.2 0.2 reshape.227
  72.5 7.9 %all_to_all.52 = bf16[4,64,288]{2,0,1:T(4,128)(2,1)S(1)} all-to-all(bf16[4,64,288]{2,0,1:T(4,128)(2,1)S(1)} %reshape.227), channel_id=1, replica_groups=mesh['grp'=2,'seq'=4,'head'=2,'sub'=2] {'head','sub'}, dimensions={1} | all-to-all | bytes 294912 | tf_op jit(solution)/shard_map/all_to_all | solution.py:78
  80.4 0.1 copy.46
  80.5 0.2 dot_general.54
  80.7 2.3 %fusion.22 = bf16[4,16,1152]{2,1,0:T(8,128)(2,1)S(1)} fusion(f32[4,16,1152]{2,1,0:T(8,128)S(1)} %bitcast.136, bf16[4,16,1152]{2,1,0:T(8,128)(2,1)S(1)} %dot_general.54, bf16[1,1152,1152]{2,1,0:T(8,128)(2,1)} %all-gather.7.cloned.1.call-done, f32[1152]{0:T(1024)S(1)} %get-tuple-element.46), kind=kOutput, calls=%fused_computation.10 | convolution fusion | flops 170090496 | bytes 3248640 | tf_op jit(solution)/shard_map/dot_general | solution.py:80
  83.0 9.0 %all_to_all.53 = bf16[4,16,1152]{2,1,0:T(8,128)(2,1)S(1)} all-to-all(bf16[4,16,1152]{2,1,0:T(8,128)(2,1)S(1)} %fusion.22), channel_id=1, replica_groups=mesh['grp'=2,'seq'=4,'head'=2,'sub'=2] {'seq'}, dimensions={0} | all-to-all | bytes 294912 | tf_op jit(solution)/shard_map/all_to_all | solution.py:97
  92.1 0.7 copy.64
  (30 shorter events, 0.5 us)
Async XLA Ops:
  6.5 3.2 %copy-start.1 = (f32[30,3,1152]{2,0,1:T(8,128)S(1)}, f32[30,3,1152]{2,0,1:T(8,128)}, u32[]{:S(2)}) copy-start(f32[30,3,1152]{2,0,1:T(8,128)} %param.9) | copy-start | bytes 1244164
  6.5 3.4 %copy-start.2 = (f32[2,3,1152]{2,0,1:T(2,128)S(1)}, f32[2,3,1152]{2,0,1:T(2,128)}, u32[]{:S(2)}) copy-start(f32[2,3,1152]{2,0,1:T(2,128)} %param.10) | copy-start | bytes 82948
  6.5 3.5 %copy-start = (bf16[1,64,1152]{2,1,0:T(8,128)(2,1)S(1)}, bf16[1,64,1152]{2,1,0:T(8,128)(2,1)}, u32[]{:S(2)}) copy-start(bf16[1,64,1152]{2,1,0:T(8,128)(2,1)} %param.7) | copy-start | bytes 442372
  6.5 32.7 %all-gather.5.cloned.1.call-start = ((), (), s32[]{:S(2)}) async-start(), calls=%async_computation.4 | async-start | bytes 3317760 | tf_op jit(solution)/shard_map/all_gather | solution.py:82
  23.6 0.9 copy-start.3
  44.1 11.1 %all-to-all-start.1 = ((bf16[4,2,9216]{2,1,0:T(2,128)(2,1)}), bf16[4,2,9216]{2,1,0:T(2,128)(2,1)S(1)}, u32[]{:S(2)}, u32[]{:S(2)}) async-start(bf16[4,2,9216]{2,1,0:T(2,128)(2,1)} %reshape.236), calls=%async_computation.1 | async-start | bytes 294912 | tf_op jit(solution)/shard_map/all_to_all | solution.py:92
  48.7 32.0 %all-gather.7.cloned.1.call-start = ((), (), s32[]{:S(2)}) async-start(), calls=%async_computation.5 | async-start | bytes 3317760 | tf_op jit(solution)/shard_map/all_gather | solution.py:82
Sparse Core Ops, SparseCore 0:
  9.2 30.0 all-gather.4
  51.0 27.7 all-gather.6
where the time goes:
time: 100 us; the launch traced here: 99.6 us
  blocking collectives  44.7 us (45%)
  between operations  14.3 us (14%)
  local copies, waits for them, and re-layouts  11.8 us (12%)
  matrix products  9.85 us (10%)
  waiting for transfers between devices  7.63 us (8%)
  other arithmetic  6.69 us (7%)
  starting transfers between devices  4.6 us (5%)
    all_gather x2, blocking collectives, gathered_heads(): lax.all_gather(normed, ('head', 'sub'), axis=1, tiled=True)  18.7 us
    all_to_all x2, blocking collectives, back_to_tokens(): lax.all_to_all(merged, ('head', 'sub'), split_axis=1, concat_axis=2, tile...  16.9 us
    all_to_all x1, blocking collectives, body(): lax.all_to_all(result, 'seq', split_axis=0, concat_axis=1, tiled=True)  9.04 us
    all_to_all x1, waiting for transfers between devices, body(): lax.all_to_all(current, 'seq', split_axis=1, concat_axis=0, tiled=True)  5.79 us
    dot_general x2, matrix products, back_to_tokens(): jnp.dot(row_block, lax.all_gather(out_weight[layer_index], ('head', 'sub'...  4.66 us
    all_to_all x1, starting transfers between devices, body(): lax.all_to_all(current, 'seq', split_axis=1, concat_axis=0, tiled=True)  4.6 us
    slice x1, local copies, waits for them, and re-layouts, gathered_heads(): qkv_weight[layer_index]  4.09 us
    dot_general x2, matrix products, project(): jnp.dot(normed.reshape(-1, normed.shape[-1]), weight.reshape(weight.shape...  3.56 us
  transfers between devices with their start and end apart: 3, of which 2 were waited for; matrix products, arithmetic and copies ran while one was open for 18% of the time, Pallas kernels for 0%

commit v1 on v0

--- a/solution.py
+++ b/solution.py
@@ -89,7 +89,9 @@
     attended = lax.map(attend, packed)
     update = back_to_tokens(attended, 0)
     current = (latents.astype(jnp.float32) + modulation[0, 2] * update).astype(jnp.bfloat16)
-    shifted_rows = lax.all_to_all(current, "seq", split_axis=1, concat_axis=0, tiled=True)
+    shards = jnp.split(current, lax.axis_size("seq"), axis=1)
+    got = lax.all_to_all(jnp.stack(shards), "seq", 0, 0)
+    shifted_rows = jnp.concatenate(got, axis=0)
     packed = gathered_heads(modulate(shifted_rows, modulation[1, 0], modulation[1, 1]), 1)
     attended = jax.vmap(attend, in_axes=1, out_axes=1)(packed)
     update = back_to_tokens(attended, 1)

time: 100 us -> 94.8 us (0.948)
  blocking collectives: 44.7 us -> 47.7 us
  other arithmetic: 6.69 us -> 3.92 us
  waiting for transfers between devices: 7.63 us -> 5.24 us
  matrix products: 9.85 us -> 8.42 us
  starting transfers between devices: 4.6 us -> 3.38 us
    all_to_all x0 -> x1, blocking collectives: none -> 11.1 us  [body(): got = lax.all_to_all(jnp.stack(shards), 'seq', 0, 0)]
    all_to_all x2 -> x1, blocking collectives: 16.9 us -> 7.67 us  [back_to_tokens(): lax.all_to_all(merged, ('head', 'sub'), split_axis=1, concat_axis=2, tile...]
    dot_general x2, matrix products: 3.56 us -> 1.98 us  [project(): jnp.dot(normed.reshape(-1, normed.shape[-1]), weight.reshape(weight.shape...]
    unnamed x2 -> x1, other arithmetic: 3.37 us -> 1.88 us
    all_to_all x1, waiting for transfers between devices: 5.79 us -> 4.48 us  [back_to_tokens(): lax.all_to_all(merged, ('head', 'sub'), split_axis=1, concat_axis=2, tile...]
    all_to_all x1, starting transfers between devices: 4.6 us -> 3.34 us  [back_to_tokens(): lax.all_to_all(merged, ('head', 'sub'), split_axis=1, concat_axis=2, tile...]
    all_gather x2, blocking collectives: 18.7 us -> 19.9 us  [gathered_heads(): lax.all_gather(normed, ('head', 'sub'), axis=1, tiled=True)]
    all_gather x2, waiting for transfers between devices: 1.1 us -> 0.04 us  [back_to_tokens(): lax.all_gather(out_weight[layer_index], ('head', 'sub'), axis=0, tiled=True)]
  transfers between devices with their start and end apart: 3 -> 3, of which waited for: 2 -> 1; matrix products, arithmetic and copies ran while one was open for 18% -> 19% of each run, Pallas kernels for 0% -> 0%
where the time goes in v1:
time: 94.8 us; the launch traced here: 94.4 us
  blocking collectives  47.7 us (50%)
  between operations  14.4 us (15%)
  local copies, waits for them, and re-layouts  11.3 us (12%)
  matrix products  8.42 us (9%)
  waiting for transfers between devices  5.24 us (6%)
  other arithmetic  3.92 us (4%)
  starting transfers between devices  3.38 us (4%)
    all_gather x2, blocking collectives, gathered_heads(): lax.all_gather(normed, ('head', 'sub'), axis=1, tiled=True)  19.9 us
    all_to_all x1, blocking collectives, body(): got = lax.all_to_all(jnp.stack(shards), 'seq', 0, 0)  11.1 us
    all_to_all x1, blocking collectives, body(): lax.all_to_all(result, 'seq', split_axis=0, concat_axis=1, tiled=True)  9.04 us
    all_to_all x1, blocking collectives, back_to_tokens(): lax.all_to_all(merged, ('head', 'sub'), split_axis=1, concat_axis=2, tile...  7.67 us
    dot_general x2, matrix products, back_to_tokens(): jnp.dot(row_block, lax.all_gather(out_weight[layer_index], ('head', 'sub'...  4.81 us
    all_to_all x1, waiting for transfers between devices, back_to_tokens(): lax.all_to_all(merged, ('head', 'sub'), split_axis=1, concat_axis=2, tile...  4.48 us
    slice x1, local copies, waits for them, and re-layouts, gathered_heads(): qkv_weight[layer_index]  4.16 us
    all_to_all x1, starting transfers between devices, back_to_tokens(): lax.all_to_all(merged, ('head', 'sub'), split_axis=1, concat_axis=2, tile...  3.34 us
  transfers between devices with their start and end apart: 3, of which 1 were waited for; matrix products, arithmetic and copies ran while one was open for 19% of the time, Pallas kernels for 0%

profile of v1, /device:TPU:0, one launch (start us, length us, event | category | flops | bytes accessed | tf_op | source)
XLA Modules:
  0.0 94.4 jit_solution(3590001869496292245)
XLA Ops:
  6.5 2.6 %fusion.68 = (bf16[1,288,1152]{2,1,0:T(8,128)(2,1)}, bf16[1,288,1152]{2,1,0:T(8,128)(2,1)}) fusion(bf16[2,288,1152]{2,1,0:T(8,128)(2,1)} %param.13), kind=kLoop, calls=%fused_computation.100 | loop fusion | bytes 2654208 | tf_op jit(solution)/shard_map/slice | solution.py:82
  9.1 0.0 all-gather.5.cloned.1.call-update
  9.8 0.1 select_reduce_fusion
  10.0 0.1 slice_reduce_fusion.1
  10.1 0.1 convert_reduce_fusion
  10.2 0.2 fusion.36
  10.4 0.1 fusion.39
  10.6 9.0 %all_gather.12 = bf16[1,256,1152]{2,1,0:T(8,128)(2,1)S(1)} all-gather(bf16[1,64,1152]{2,1,0:T(8,128)(2,1)S(1)} %fusion.39), channel_id=1, replica_groups=mesh['grp'=2,'seq'=4,'head'=2,'sub'=2] {'head','sub'}, dimensions={1}, use_global_device_ids=true | all-gather | bytes 737280 | tf_op jit(solution)/shard_map/all_gather | solution.py:71
  19.6 4.2 %fusion.67 = (bf16[1,1152,4,216]{1,3,2,0:T(8,128)(2,1)S(1)}, bf16[1,1152,4,216]{1,3,2,0:T(8,128)(2,1)}) fusion(bf16[2,1152,4,216]{1,3,2,0:T(8,128)(2,1)} %param.11), kind=kLoop, calls=%fused_computation.99 | loop fusion | bytes 7962624 | tf_op jit(solution)/shard_map/slice | solution.py:72
  23.7 0.8 convolution_bitcast_fusion
  24.5 0.1 multiply_reduce_fusion.3
  24.6 0.0 copy-done.4
  24.6 0.4 fusion.25
  25.0 0.3 convolution_convert_fusion.1
  25.4 0.4 copy.34
  25.8 0.5 broadcast.174
  26.3 1.9 %reduce.19 = bf16[256,288]{1,0:T(8,128)(2,1)S(1)} reduce(bf16[256,1,288]{2,1,0:T(2,128)(2,1)S(1)} %bitcast.155, bf16[]{:T(256)} %broadcast.174), dimensions={1}, to_apply=%bitcast.143.reduce_sub_computation | reduce | bytes 294914
  28.2 1.0 %reshape.220 = bf16[4,2,9216]{2,1,0:T(2,128)(2,1)} reshape(bf16[256,288]{1,0:T(8,128)(2,1)S(1)} %reduce.19) | data formatting | bytes 294912
  29.2 3.3 %all-to-all-start = ((bf16[4,2,9216]{2,1,0:T(2,128)(2,1)}), bf16[4,2,9216]{2,1,0:T(2,128)(2,1)S(1)}, u32[]{:S(2)}, u32[]{:S(2)}) async-start(bf16[4,2,9216]{2,1,0:T(2,128)(2,1)} %reshape.220), calls=%async_computation | async-start | bytes 294912 | tf_op jit(solution)/shard_map/all_to_all | solution.py:78
  32.5 0.0 all-gather.7.cloned.1.call-start
  32.6 0.7 all-gather.7.cloned.1.call-update
  33.3 4.5 %all-to-all-done = bf16[4,2,9216]{2,1,0:T(2,128)(2,1)S(1)} async-done(((bf16[4,2,9216]{2,1,0:T(2,128)(2,1)}), bf16[4,2,9216]{2,1,0:T(2,128)(2,1)S(1)}, u32[]{:S(2)}, u32[]{:S(2)}) %all-to-all-start) | async-done | bytes 147488 | tf_op jit(solution)/shard_map/all_to_all | solution.py:78
  37.8 0.4 reshape.221
  38.2 0.2 copy.35
  38.3 0.2 reshape.205
  38.5 0.0 all-gather.5.cloned.1.call-done
  38.5 2.5 %fusion.19 = bf16[1,64,1152]{2,1,0:T(8,128)(2,1)S(1)} fusion(bf16[64,1152]{1,0:T(8,128)(2,1)S(1)} %reshape.205, bf16[1,1152,1152]{2,1,0:T(8,128)(2,1)} %all-gather.5.cloned.1.call-done, bf16[1,64,1152]{2,1,0:T(8,128)(2,1)S(1)} %copy-done, f32[1152]{0:T(1024)S(1)} %get-tuple-element.58), kind=kOutput, calls=%fused_computation.9 | convolution fusion | flops 170164224 | bytes 3101184 | tf_op jit(solution)/shard_map/dot_general | solution.py:80
  41.1 11.1 %all_to_all.47 = bf16[4,1,16,1152]{3,2,1,0:T(8,128)(2,1)S(1)} all-to-all(bf16[4,1,16,1152]{3,2,1,0:T(8,128)(2,1)S(1)} %pad_maximum_fusion), channel_id=1, replica_groups=mesh['grp'=2,'seq'=4,'head'=2,'sub'=2] {'seq'}, dimensions={0} | all-to-all | bytes 294912 | tf_op jit(solution)/shard_map/all_to_all | solution.py:93
  52.1 0.1 convert_reduce_fusion.1
  52.3 0.2 fusion.40
  52.4 0.1 fusion.43
  52.6 10.9 %all_gather.14 = bf16[4,64,1152]{2,1,0:T(8,128)(2,1)S(1)} all-gather(bf16[4,16,1152]{2,1,0:T(8,128)(2,1)S(1)} %fusion.43), channel_id=1, replica_groups=mesh['grp'=2,'seq'=4,'head'=2,'sub'=2] {'head','sub'}, dimensions={1}, use_global_device_ids=true | all-gather | bytes 737280 | tf_op jit(solution)/shard_map/all_gather | solution.py:71
  63.5 1.2 %fusion.27 = f32[4,64,4,3,72]{4,1,3,2,0:T(8,128)S(1)} fusion(bf16[4,3,72,1152,1]{3,2,1,0,4:T(8,128)(2,1)S(1)} %bitcast.153, bf16[4,64,1152]{2,1,0:T(8,128)(2,1)S(1)} %all_gather.14), kind=kOutput, calls=%fused_computation.18 | convolution fusion | flops 509607936 | bytes 3465216 | tf_op jit(solution)/shard_map/dot_general | solution.py:29
  64.7 0.4 multiply_reduce_fusion.1
  65.1 0.3 fusion.48
  65.5 0.5 fusion.52
  65.9 0.3 copy.38
  66.3 0.3 copy.40
  66.7 0.4 fusion.26
  67.1 0.1 copy.48
  67.2 0.2 reshape.213
  67.5 7.7 %all_to_all.48 = bf16[4,64,288]{2,0,1:T(4,128)(2,1)S(1)} all-to-all(bf16[4,64,288]{2,0,1:T(4,128)(2,1)S(1)} %reshape.213), channel_id=1, replica_groups=mesh['grp'=2,'seq'=4,'head'=2,'sub'=2] {'head','sub'}, dimensions={1} | all-to-all | bytes 294912 | tf_op jit(solution)/shard_map/all_to_all | solution.py:78
  75.2 0.1 copy.44
  75.3 0.2 dot_general.54
  75.4 0.0 all-gather.7.cloned.1.call-done
  75.5 2.3 %fusion.22 = bf16[4,16,1152]{2,1,0:T(8,128)(2,1)S(1)} fusion(bf16[4,16,1152]{2,1,0:T(8,128)(2,1)S(1)} %dot_general.54, bf16[1,1152,1152]{2,1,0:T(8,128)(2,1)} %all-gather.7.cloned.1.call-done, bf16[4,1,16,1152]{3,2,1,0:T(8,128)(2,1)S(1)} %all_to_all.47, f32[1152]{0:T(1024)S(1)} %get-tuple-element.46), kind=kOutput, calls=%fused_computation.10 | convolution fusion | flops 170164224 | bytes 3101184 | tf_op jit(solution)/shard_map/dot_general | solution.py:80
  77.8 9.0 %all_to_all.49 = bf16[4,16,1152]{2,1,0:T(8,128)(2,1)S(1)} all-to-all(bf16[4,16,1152]{2,1,0:T(8,128)(2,1)S(1)} %fusion.22), channel_id=1, replica_groups=mesh['grp'=2,'seq'=4,'head'=2,'sub'=2] {'seq'}, dimensions={0} | all-to-all | bytes 294912 | tf_op jit(solution)/shard_map/all_to_all | solution.py:99
  86.8 0.7 copy.59
  (27 shorter events, 0.3 us)
Async XLA Ops:
  6.5 3.3 %copy-start.2 = (f32[30,3,1152]{2,0,1:T(8,128)S(1)}, f32[30,3,1152]{2,0,1:T(8,128)}, u32[]{:S(2)}) copy-start(f32[30,3,1152]{2,0,1:T(8,128)} %param.9) | copy-start | bytes 1244164
  6.5 3.4 %copy-start.3 = (f32[2,3,1152]{2,0,1:T(2,128)S(1)}, f32[2,3,1152]{2,0,1:T(2,128)}, u32[]{:S(2)}) copy-start(f32[2,3,1152]{2,0,1:T(2,128)} %param.10) | copy-start | bytes 82948
  6.5 3.5 %copy-start = (bf16[1,64,1152]{2,1,0:T(8,128)(2,1)S(1)}, bf16[1,64,1152]{2,1,0:T(8,128)(2,1)}, u32[]{:S(2)}) copy-start(bf16[1,64,1152]{2,1,0:T(8,128)(2,1)} %param.7) | copy-start | bytes 442372
  6.5 32.0 %all-gather.5.cloned.1.call-start = ((), (), s32[]{:S(2)}) async-start(), calls=%async_computation.4 | async-start | bytes 3317760 | tf_op jit(solution)/shard_map/all_gather | solution.py:82
  23.7 0.9 copy-start.4
  29.2 8.6 %all-to-all-start = ((bf16[4,2,9216]{2,1,0:T(2,128)(2,1)}), bf16[4,2,9216]{2,1,0:T(2,128)(2,1)S(1)}, u32[]{:S(2)}, u32[]{:S(2)}) async-start(bf16[4,2,9216]{2,1,0:T(2,128)(2,1)} %reshape.220), calls=%async_computation | async-start | bytes 294912 | tf_op jit(solution)/shard_map/all_to_all | solution.py:78
  32.5 42.9 %all-gather.7.cloned.1.call-start = ((), (), s32[]{:S(2)}) async-start(), calls=%async_computation.5 | async-start | bytes 3317760 | tf_op jit(solution)/shard_map/all_gather | solution.py:82
  38.5 25.0 %copy-start.1 = (bf16[1,1152,4,216]{1,3,2,0:T(8,128)(2,1)S(1)}, bf16[1,1152,4,216]{1,3,2,0:T(8,128)(2,1)}, u32[]{:S(2)}) copy-start(bf16[1,1152,4,216]{1,3,2,0:T(8,128)(2,1)} %get-tuple-element.60) | copy-start | bytes 5971972
Sparse Core Ops, SparseCore 0:
  9.3 28.9 all-gather.4
  39.8 28.8 all-gather.6
